TPU v7x, 32 devices: a whole 2x2x4 slice. The times are simulated.
32 devices in a mesh: fsdp: 8 (over z, y), seq: 4 (over x, core).
Axes of the slice: x: 2, y: 2, z: 4, core: 2. Of those that a mesh axis runs over, the one named last changes fastest.
Arguments:
- tokens: bfloat16 [8, 1024, 768], P('fsdp', 'seq'), may hold values from -6 to 6
- condition: bfloat16 [8, 768], P('fsdp'), may hold values from -6 to 6
- ada_weight: bfloat16 [2, 768, 4608], P(None, 'fsdp'), may hold values from -0.21875 to 0.21875
- ada_bias: bfloat16 [2, 4608], P(None, 'fsdp'), may hold values from -3 to 3
- qkv_weight: bfloat16 [2, 768, 2304], P(None, 'fsdp'), may hold values from -0.21875 to 0.21875
- qv_bias: bfloat16 [2, 1536], P(None, 'fsdp'), may hold values from -3 to 3
- out_weight: bfloat16 [2, 768, 768], P(None, 'fsdp'), may hold values from -1.25 to 1.25
- out_bias: bfloat16 [2, 768], P(None, 'fsdp'), may hold values from -3 to 3
- up_weight: bfloat16 [2, 768, 3072], P(None, 'fsdp'), may hold values from -0.21875 to 0.21875
- up_bias: bfloat16 [2, 3072], P(None, 'fsdp'), may hold values from -3 to 3
- down_weight: bfloat16 [2, 3072, 768], P(None, 'fsdp'), may hold values from -0.109375 to 0.109375
- down_bias: bfloat16 [2, 768], P(None, 'fsdp'), may hold values from -3 to 3
- cotangent: bfloat16 [8, 1024, 768], P('fsdp', 'seq'), may hold values from -6 to 6
Outputs:
- block_out: bfloat16 [8, 1024, 768], P('fsdp', 'seq')
- grad_tokens: float32 [8, 1024, 768], P('fsdp', 'seq')
- grad_condition: float32 [8, 768], P('fsdp')
- grad_ada_weight: float32 [2, 768, 4608], P(None, 'fsdp')
- grad_ada_bias: float32 [2, 4608], P(None, 'fsdp')
- grad_qkv_weight: float32 [2, 768, 2304], P(None, 'fsdp')
- grad_qv_bias: float32 [2, 1536], P(None, 'fsdp')
- grad_out_weight: float32 [2, 768, 768], P(None, 'fsdp')
- grad_out_bias: float32 [2, 768], P(None, 'fsdp')
- grad_up_weight: float32 [2, 768, 3072], P(None, 'fsdp')
- grad_up_bias: float32 [2, 3072], P(None, 'fsdp')
- grad_down_weight: float32 [2, 3072, 768], P(None, 'fsdp')
- grad_down_bias: float32 [2, 768], P(None, 'fsdp')
All inputs are finite; a program needn't handle non-finite values.
Results may differ from a plain program's by a relative error of at most 0.017.
The roundings to bfloat16 on the way count: a program that leaves them out, or rounds other values in their place, can miss the bound.
Values may be sent and summed in bfloat16 or wider, within the bound.
A program may use at most 256 MiB of HBM per device.

v0:
```python
import jax
import jax.numpy as jnp
from jax import lax
from jax.sharding import PartitionSpec as P

HEAD_DIM = 64
SCORE_SCALE = HEAD_DIM ** (-0.5)
EPSILON = 1e-06
HIGHEST = lax.Precision.HIGHEST
F32 = jnp.float32
BF16 = jnp.bfloat16


def normalize(values):
    centred = values - jnp.mean(values, axis=-1, keepdims=True)
    inverse = lax.rsqrt(jnp.mean(centred * centred, axis=-1, keepdims=True) + EPSILON)
    return (centred * inverse, inverse)


def norm_back(gradient, normed, inverse):
    return inverse * (
        gradient
        - jnp.mean(gradient, axis=-1, keepdims=True)
        - normed * jnp.mean(gradient * normed, axis=-1, keepdims=True)
    )


def mm(a, b):
    return lax.dot_general(a, b, (((1,), (0,)), ((), ())), preferred_element_type=F32)


def mm_nt(a, b):
    return lax.dot_general(a, b, (((1,), (1,)), ((), ())), preferred_element_type=F32)


def mm_tn(a, b):
    return lax.dot_general(a, b, (((0,), (0,)), ((), ())), preferred_element_type=F32)


def split_heads(rows):
    return rows.reshape(rows.shape[0], -1, HEAD_DIM).transpose(1, 0, 2)


def join_heads(heads):
    return heads.transpose(1, 0, 2).reshape(heads.shape[1], -1)


def attend(q, k, v):
    q, k, v = (split_heads(q), split_heads(k), split_heads(v))
    scores = jnp.einsum("hqd,hkd->hqk", q, k, preferred_element_type=F32) * SCORE_SCALE
    logsum = jnp.log(jnp.sum(jnp.exp(scores), axis=-1, keepdims=True))
    prob = jnp.exp(scores - logsum).astype(BF16)
    out = jnp.einsum("hqk,hkd->hqd", prob, v, preferred_element_type=F32)
    return (join_heads(out).astype(BF16), logsum)


def attend_back(q, k, v, logsum, out_grad):
    q, k, v, out_grad = (split_heads(q), split_heads(k), split_heads(v), split_heads(out_grad))
    scores = jnp.einsum("hqd,hkd->hqk", q, k, preferred_element_type=F32) * SCORE_SCALE
    prob = jnp.exp(scores - logsum)
    dv = jnp.einsum("hqk,hqd->hkd", prob.astype(BF16), out_grad, preferred_element_type=F32)
    dp = jnp.einsum("hqd,hkd->hqk", out_grad, v, preferred_element_type=F32)
    inner = jnp.sum(prob * dp, axis=-1, keepdims=True)
    ds = (prob * (dp - inner)).astype(BF16)
    dq = jnp.einsum("hqk,hkd->hqd", ds, k, preferred_element_type=F32) * SCORE_SCALE
    dk = jnp.einsum("hqk,hqd->hkd", ds, q, preferred_element_type=F32) * SCORE_SCALE
    return [join_heads(t).astype(BF16) for t in (dq, dk, dv)]


def gelu_parts(u):
    c = 0.7978845608028654
    inner = c * (u + 0.044715 * (u * u * u))
    t = jnp.tanh(inner)
    value = 0.5 * u * (1.0 + t)
    slope = 0.5 * (1.0 + t) + 0.5 * u * (1.0 - t * t) * (c * (1.0 + 3.0 * 0.044715 * u * u))
    return (value, slope)


def per_device(
    tokens,
    condition,
    ada_weight,
    ada_bias,
    qkv_weight,
    qv_bias,
    out_weight,
    out_bias,
    up_weight,
    up_bias,
    down_weight,
    down_bias,
    cotangent,
):
    n = lax.axis_size("fsdp")
    ns = lax.axis_size("seq")
    f = lax.axis_index("fsdp")
    s = lax.axis_index("seq")
    layers, rows, width6 = ada_weight.shape
    width = rows * n
    ff = up_weight.shape[2]
    hc = width // ns
    fc = ff // (ns * n)

    def take(x, axis):
        return lax.dynamic_index_in_dim(x, s, axis, keepdims=False)

    def own(x, axis, size):
        return lax.dynamic_slice_in_dim(x, f * size, size, axis)

    w_qkv, w_rest = ([], [])
    for l in range(layers):
        q_part = take(qkv_weight[l].reshape(rows, 3, ns, hc), 2).reshape(rows, 3 * hc)
        u_part = take(up_weight[l].reshape(rows, n, ns, fc), 2).reshape(rows, n * fc)
        d_part = take(down_weight[l].reshape(ns, fc, width), 0)
        w_qkv.append(lax.all_gather(q_part, "fsdp", axis=0, tiled=True))
        rest = jnp.concatenate([u_part, d_part, out_weight[l]], axis=1)
        w_rest.append(lax.all_gather(rest, "fsdp", axis=0, tiled=True))
    fw = n * fc
    cond_float = condition.astype(F32)
    cond_act = jax.nn.silu(cond_float).astype(BF16)
    small = jnp.concatenate(
        [
            ada_bias.reshape(-1),
            qv_bias.reshape(-1),
            out_bias.reshape(-1),
            up_bias.reshape(-1),
            down_bias.reshape(-1),
            cond_act.reshape(-1),
        ]
    )
    small = lax.all_gather(small, "fsdp", axis=0, tiled=False)
    pos = 0

    def unpack(per_layer):
        nonlocal pos
        part = small[:, pos : pos + layers * per_layer].reshape(n, layers, per_layer)
        pos += layers * per_layer
        return part.transpose(1, 0, 2).reshape(layers, n * per_layer)

    ada_b = unpack(ada_bias.shape[1]).astype(F32)
    qv_b = unpack(qv_bias.shape[1]).astype(F32)
    out_b = unpack(out_bias.shape[1]).astype(F32)
    up_b = unpack(up_bias.shape[1]).astype(F32)
    down_b = unpack(down_bias.shape[1]).astype(F32)
    cond_all = small[:, pos:]
    cond_rows = own(cond_all, 1, rows)
    q_b = take(qv_b[:, :width].reshape(layers, ns, hc), 1)
    v_b = take(qv_b[:, width:].reshape(layers, ns, hc), 1)
    qkv_b = jnp.concatenate([q_b, jnp.zeros_like(q_b), v_b], axis=1)
    up_bs = take(up_b.reshape(layers, n, ns, fc), 2).reshape(layers, fw)
    mod_partial = jnp.stack([mm(cond_rows, ada_weight[l]) for l in range(layers)], axis=1)
    mod = lax.psum_scatter(mod_partial, "fsdp", scatter_dimension=0, tiled=True)[0] + ada_b
    hidden = tokens[0].astype(F32)
    saved = []
    for l in range(layers):
        shift_a, scale_a, gate_a, shift_m, scale_m, gate_m = jnp.split(mod[l], 6)
        n_a, r_a = normalize(hidden)
        attn_in = (n_a * (1.0 + scale_a) + shift_a).astype(BF16)
        attn_all = lax.all_gather(attn_in, "seq", axis=0, tiled=True)
        qkv = (mm(attn_all, w_qkv[l]) + qkv_b[l]).astype(BF16)
        q, k, v = (qkv[:, :hc], qkv[:, hc : 2 * hc], qkv[:, 2 * hc :])
        head_out, logsum = attend(q, k, v)
        tok_out = lax.all_to_all(head_out, "seq", split_axis=0, concat_axis=1, tiled=True)
        branch = mm(tok_out, w_rest[l][:, fw + width :]) + out_b[l]
        middle = hidden + gate_a * branch
        n_m, r_m = normalize(middle)
        mlp_in = (n_m * (1.0 + scale_m) + shift_m).astype(BF16)
        mlp_all = lax.all_gather(mlp_in, "seq", axis=0, tiled=True)
        up = mm(mlp_all, w_rest[l][:, :fw]) + up_bs[l]
        act = gelu_parts(up)[0].astype(BF16)
        feed = mm(act, w_rest[l][:, fw : fw + width])
        feed = lax.psum_scatter(feed, "seq", scatter_dimension=0, tiled=True) + down_b[l]
        saved.append(
            (n_a, r_a, attn_all, q, k, v, logsum, tok_out, branch, n_m, r_m, mlp_all, up, act, feed)
        )
        hidden = middle + gate_m * feed
    block_out = hidden.astype(BF16)
    g = cotangent[0].astype(F32)
    d_mods = [None] * layers
    reduced = [None] * layers
    bias_grads = [None] * layers
    for l in reversed(range(layers)):
        shift_a, scale_a, gate_a, shift_m, scale_m, gate_m = jnp.split(mod[l], 6)
        n_a, r_a, attn_all, q, k, v, logsum, tok_out, branch, n_m, r_m, mlp_all, up, act, feed = (
            saved[l]
        )
        g_feed = (gate_m * g).astype(BF16)
        d_gate_m = jnp.sum(g * feed, axis=0)
        g_feed_all = lax.all_gather(g_feed, "seq", axis=0, tiled=True)
        grad_down = mm_tn(act, g_feed_all)
        g_up = (mm_nt(g_feed_all, w_rest[l][:, fw : fw + width]) * gelu_parts(up)[1]).astype(BF16)
        grad_up = mm_tn(mlp_all, g_up)
        g_min = lax.psum_scatter(
            mm_nt(g_up, w_rest[l][:, :fw]), "seq", scatter_dimension=0, tiled=True
        )
        d_scale_m = jnp.sum(g_min * n_m, axis=0)
        d_shift_m = jnp.sum(g_min, axis=0)
        g_mid = g + norm_back(g_min * (1.0 + scale_m), n_m, r_m)
        g_branch = (gate_a * g_mid).astype(BF16)
        d_gate_a = jnp.sum(g_mid * branch, axis=0)
        grad_out = mm_tn(tok_out, g_branch)
        g_o = mm_nt(g_branch, w_rest[l][:, fw + width :]).astype(BF16)
        g_o_heads = lax.all_to_all(g_o, "seq", split_axis=1, concat_axis=0, tiled=True)
        dq, dk, dv = attend_back(q, k, v, logsum, g_o_heads)
        g_qkv = jnp.concatenate([dq, dk, dv], axis=1)
        grad_qkv = mm_tn(attn_all, g_qkv)
        g_ain = lax.psum_scatter(mm_nt(g_qkv, w_qkv[l]), "seq", scatter_dimension=0, tiled=True)
        d_scale_a = jnp.sum(g_ain * n_a, axis=0)
        d_shift_a = jnp.sum(g_ain, axis=0)
        g = g_mid + norm_back(g_ain * (1.0 + scale_a), n_a, r_a)
        d_mods[l] = jnp.concatenate(
            [d_shift_a, d_scale_a, d_gate_a, d_shift_m, d_scale_m, d_gate_m]
        )
        packed = jnp.concatenate([grad_up, grad_down, grad_out, grad_qkv], axis=1).astype(BF16)
        reduced[l] = lax.psum_scatter(packed, "fsdp", scatter_dimension=0, tiled=True)

        def place(x, axis):
            zeros = jnp.zeros(x.shape[:axis] + (ns,) + x.shape[axis + 1 :], F32)
            return lax.dynamic_update_slice_in_dim(zeros, x, s, axis)

        qv_g = place(
            jnp.stack([jnp.sum(dq.astype(F32), axis=0), jnp.sum(dv.astype(F32), axis=0)])[
                :, None, :
            ],
            1,
        )
        up_g = place(jnp.sum(g_up.astype(F32), axis=0).reshape(n, 1, fc), 1)
        bias_grads[l] = jnp.concatenate(
            [
                qv_g.reshape(n, -1),
                jnp.sum(g_branch.astype(F32), axis=0).reshape(n, -1),
                up_g.reshape(n, -1),
                jnp.sum(g_feed.astype(F32), axis=0).reshape(n, -1),
            ],
            axis=1,
        )
    red = jnp.stack(reduced)
    shared = jnp.concatenate([red[:, :, : fw + width], red[:, :, fw + 2 * width :]], axis=2)
    shared = lax.all_gather(shared, "seq", axis=0, tiled=False).astype(F32)
    grad_up = (
        shared[..., :fw]
        .reshape(ns, layers, rows, n, fc)
        .transpose(1, 2, 3, 0, 4)
        .reshape(layers, rows, ff)
    )
    grad_down = shared[..., fw : fw + width].transpose(1, 0, 2, 3).reshape(layers, ns * fc, width)
    grad_qkv = shared[..., fw + width :].reshape(ns, layers, rows, 3, hc).transpose(1, 2, 3, 0, 4)
    grad_qkv = grad_qkv.reshape(layers, rows, 3 * width)
    grad_out = lax.psum(red[:, :, fw + width : fw + 2 * width], "seq").astype(F32)
    bias = lax.psum(jnp.stack(bias_grads), ("fsdp", "seq"))
    bias = lax.dynamic_index_in_dim(bias, f, 1, keepdims=False)
    cuts = [qv_bias.shape[1], out_bias.shape[1], up_bias.shape[1], down_bias.shape[1]]
    grad_bias, at = ([], 0)
    for size in cuts:
        grad_bias.append(bias[:, at : at + size])
        at += size
    d_mod = lax.psum(jnp.stack(d_mods), "seq")
    d_mod_all = lax.all_gather(d_mod, "fsdp", axis=0, tiled=False)
    cond_rows32 = cond_rows.astype(F32)
    grad_ada = jnp.stack(
        [
            lax.dot_general(
                cond_rows32,
                d_mod_all[:, l],
                (((0,), (0,)), ((), ())),
                precision=HIGHEST,
                preferred_element_type=F32,
            )
            for l in range(layers)
        ]
    )
    grad_ada_bias = own(jnp.sum(d_mod_all, axis=0), 1, width6 // n)
    g_cond = sum(
        (
            lax.dot_general(
                d_mod_all[:, l],
                ada_weight[l].astype(F32),
                (((1,), (1,)), ((), ())),
                precision=HIGHEST,
                preferred_element_type=F32,
            )
            for l in range(layers)
        )
    )
    g_cond = lax.all_to_all(g_cond, "fsdp", split_axis=0, concat_axis=1, tiled=True)
    _, silu_back = jax.vjp(jax.nn.silu, cond_float)
    grad_condition = silu_back(g_cond)[0]
    return (
        block_out[None],
        g[None],
        grad_condition,
        grad_ada,
        grad_ada_bias,
        grad_qkv,
        grad_bias[0],
        grad_out,
        grad_bias[1],
        grad_up,
        grad_bias[2],
        grad_down,
        grad_bias[3],
    )


def solution(mesh):
    token = P("fsdp", "seq", None)
    matrix = P(None, "fsdp", None)
    vector = P(None, "fsdp")
    return jax.shard_map(
        per_device,
        mesh=mesh,
        in_specs=(token, P("fsdp", None)) + (matrix, vector) * 5 + (token,),
        out_specs=(token, token, P("fsdp", None)) + (matrix, vector) * 5,
        check_vma=False,
    )
```

profile of v0, /device:TPU:0, one launch (start us, length us, event | category | flops | bytes accessed | tf_op | source)
XLA Modules:
  0.0 1008.6 jit_solution(16156190823706369313)
XLA Ops:
  12.4 32.4 %all-gather.2 = bf16[8,1,3456]{2,1,0:T(2,128)(2,1)S(1)} all-gather(bf16[1,1,3456]{2,1,0:T(2,128)(2,1)S(1)} %reshape.391), channel_id=2, replica_groups=mesh['fsdp'=8,'seq'=4] {'fsdp'}, dimensions={0}, use_global_device_ids=true | all-gather | bytes 62208 | tf_op jit(solution)/shard_map/all_gather | solution.py:131
  50.2 71.0 %all-reduce.6.cloned.1.call-done = f32[8,2,4608]{2,1,0:T(2,128)} async-done(((f32[8,2,4608]{2,1,0:T(2,128)}), f32[8,2,4608]{2,1,0:T(2,128)}) %all-reduce.6.cloned.1.call-update) | async-done | bytes 294928
  135.6 34.4 %all_gather.51 = bf16[768,576]{1,0:T(8,128)(2,1)S(1)} all-gather(bf16[96,576]{1,0:T(8,128)(2,1)S(1)} %copy.123), channel_id=1, replica_groups=mesh['fsdp'=8,'seq'=4] {'fsdp'}, dimensions={0}, use_global_device_ids=true | all-gather | bytes 995328 | tf_op jit(solution)/shard_map/all_gather | solution.py:115
  197.6 14.9 %all-gather.15.cloned.1.call-done = bf16[768,2304]{1,0:T(8,128)(2,1)} async-done(((bf16[96,2304]{1,0:T(8,128)(2,1)}), bf16[768,2304]{1,0:T(8,128)(2,1)}) %all-gather.15.cloned.1.call-update) | async-done | bytes 3538960 | tf_op jit(solution)/shard_map/all_gather | solution.py:117
  216.7 18.2 %all-gather.17.cloned.1.call-done = bf16[1024,768]{1,0:T(8,128)(2,1)} async-done(((bf16[256,768]{1,0:T(8,128)(2,1)}), bf16[1024,768]{1,0:T(8,128)(2,1)}) %all-gather.17.cloned.1.call-update) | async-done | bytes 1572880 | tf_op jit(solution)/shard_map/all_gather | solution.py:168
  244.9 37.9 %reduce-scatter.13.cloned.1.call-done = f32[256,768]{1,0:T(8,128)} async-done(((f32[1024,768]{1,0:T(8,128)}), f32[256,768]{1,0:T(8,128)}) %reduce-scatter.13.cloned.1.call-update) | async-done | bytes 786448 | tf_op jit(solution)/shard_map/reduce_scatter | solution.py:172
  289.8 32.9 %all_gather.55 = bf16[768,576]{1,0:T(8,128)(2,1)S(1)} all-gather(bf16[96,576]{1,0:T(8,128)(2,1)S(1)} %copy.129), channel_id=1, replica_groups=mesh['fsdp'=8,'seq'=4] {'fsdp'}, dimensions={0}, use_global_device_ids=true | all-gather | bytes 995328 | tf_op jit(solution)/shard_map/all_gather | solution.py:115
  343.8 28.8 %all-gather.21.cloned.1.call-done = bf16[768,2304]{1,0:T(8,128)(2,1)} async-done(((bf16[96,2304]{1,0:T(8,128)(2,1)}), bf16[768,2304]{1,0:T(8,128)(2,1)}) %all-gather.21.cloned.1.call-update) | async-done | bytes 3538960 | tf_op jit(solution)/shard_map/all_gather | solution.py:117
  377.7 17.5 %all-gather.23.cloned.1.call-done = bf16[1024,768]{1,0:T(8,128)(2,1)} async-done(((bf16[256,768]{1,0:T(8,128)(2,1)}), bf16[1024,768]{1,0:T(8,128)(2,1)}) %all-gather.23.cloned.1.call-update) | async-done | bytes 1572880 | tf_op jit(solution)/shard_map/all_gather | solution.py:168
  400.0 17.0 %all-gather.25.cloned.1.call-done = bf16[1024,768]{1,0:T(8,128)(2,1)} async-done(((bf16[256,768]{1,0:T(8,128)(2,1)}), bf16[1024,768]{1,0:T(8,128)(2,1)}) %all-gather.25.cloned.1.call-update) | async-done | bytes 1572880 | tf_op jit(solution)/shard_map/all_gather | solution.py:189
  434.2 31.9 %reduce-scatter.17.cloned.1.call-done = f32[256,768]{1,0:T(8,128)} async-done(((f32[1024,768]{1,0:T(8,128)}), f32[256,768]{1,0:T(8,128)}) %reduce-scatter.17.cloned.1.call-update) | async-done | bytes 786448 | tf_op jit(solution)/shard_map/reduce_scatter | solution.py:193
  467.6 38.9 %reduce-scatter.15.cloned.1.call-done = f32[256,768]{1,0:T(8,128)} async-done(((f32[1024,768]{1,0:T(8,128)}), f32[256,768]{1,0:T(8,128)}) %reduce-scatter.15.cloned.1.call-update) | async-done | bytes 786448 | tf_op jit(solution)/shard_map/reduce_scatter | solution.py:172
  511.5 10.2 %all_to_all.80 = bf16[256,4,192]{0,2,1:T(8,128)(2,1)S(1)} all-to-all(bf16[256,4,192]{0,2,1:T(8,128)(2,1)S(1)} %bitcast.284), channel_id=1, replica_groups=mesh['fsdp'=8,'seq'=4] {'seq'}, dimensions={1} | all-to-all | bytes 786432 | tf_op jit(solution)/shard_map/all_to_all | solution.py:203
  553.4 38.0 %reduce-scatter.19.cloned.1.call-done = f32[256,768]{1,0:T(8,128)} async-done(((f32[1024,768]{1,0:T(8,128)}), f32[256,768]{1,0:T(8,128)}) %reduce-scatter.19.cloned.1.call-update) | async-done | bytes 786448 | tf_op jit(solution)/shard_map/reduce_scatter | solution.py:207
  595.5 19.6 %all-gather.27.cloned.1.call-done = bf16[1024,768]{1,0:T(8,128)(2,1)} async-done(((bf16[256,768]{1,0:T(8,128)(2,1)}), bf16[1024,768]{1,0:T(8,128)(2,1)}) %all-gather.27.cloned.1.call-update) | async-done | bytes 1572880 | tf_op jit(solution)/shard_map/all_gather | solution.py:189
  643.2 21.0 %reduce-scatter.21.cloned.1.call-done = f32[256,768]{1,0:T(8,128)} async-done(((f32[1024,768]{1,0:T(8,128)}), f32[256,768]{1,0:T(8,128)}) %reduce-scatter.21.cloned.1.call-update) | async-done | bytes 786448 | tf_op jit(solution)/shard_map/reduce_scatter | solution.py:193
  670.2 10.0 all_to_all.81
  680.8 11.1 %multiply_reduce_fusion = (f32[3,1024]{1,0:T(4,128)S(1)}, f32[3,1024,1024]{1,2,0:T(8,128)}) fusion(f32[3,1024,1024]{1,2,0:T(8,128)} %fusion.3, bf16[3,1024,64]{1,2,0:T(8,128)(2,1)S(1)} %bitcast.272, bf16[1024,3,64]{0,2,1:T(8,128)(2,1)S(1)} %reshape.363), kind=kOutput, calls=%fused_computation.7 | convolution fusion | flops 408941568 | bytes 25964544 | tf_op jit(solution)/shard_map/hqd,hkd->hqk/dot_general | solution.py:62
  691.9 10.3 %multiply_convert_fusion = bf16[3,1024,1024]{1,2,0:T(8,128)(2,1)S(1)} fusion(f32[3,1024,1024]{1,2,0:T(8,128)} %fusion.3, f32[3,1024,1024]{1,2,0:T(8,128)} %get-tuple-element.173, f32[3,1024]{1,0:T(4,128)S(1)} %get-tuple-element.172), kind=kLoop, calls=%fused_computation.6 | loop fusion | flops 9437184 | bytes 31469568 | tf_op jit(solution)/shard_map/convert_element_type | solution.py:64
  728.6 32.6 %reduce-scatter.27.cloned.1.call-done = bf16[96,2880]{1,0:T(8,128)(2,1)} async-done(((bf16[768,2880]{1,0:T(8,128)(2,1)}), bf16[96,2880]{1,0:T(8,128)(2,1)}) %reduce-scatter.27.cloned.1.call-update) | async-done | bytes 552976
  763.2 40.9 %psum.22 = f32[2,8,768]{2,0,1:T(2,128)S(1)} all-reduce(f32[2,8,768]{2,0,1:T(2,128)S(1)} %pad_maximum_fusion.14), channel_id=1, replica_groups=mesh['fsdp'=8,'seq'=4] {'fsdp','seq'}, use_global_device_ids=true, to_apply=%region_53.54 | all-reduce | flops 12288 | bytes 98304 | tf_op jit(solution)/shard_map/psum | solution.py:250
  807.6 92.1 %reduce-scatter.25.cloned.1.call-done = bf16[96,2880]{1,0:T(8,128)(2,1)} async-done(((bf16[768,2880]{1,0:T(8,128)(2,1)}), bf16[96,2880]{1,0:T(8,128)(2,1)}) %reduce-scatter.25.cloned.1.call-update) | async-done | bytes 552976
  908.4 11.1 %psum.21 = f32[1,2,4608]{2,1,0:T(2,128)S(1)} all-reduce(f32[1,2,4608]{2,1,0:T(2,128)S(1)} %maximum_bitcast_fusion), channel_id=1, replica_groups=mesh['fsdp'=8,'seq'=4] {'seq'}, use_global_device_ids=true, to_apply=%region_39.40 | all-reduce | flops 9216 | bytes 73728 | tf_op jit(solution)/shard_map/psum | solution.py:257
  919.5 31.0 %all_gather.61 = f32[8,2,4608]{2,1,0:T(2,128)S(1)} all-gather(f32[1,2,4608]{2,1,0:T(2,128)S(1)} %psum.21), channel_id=1, replica_groups=mesh['fsdp'=8,'seq'=4] {'fsdp'}, dimensions={0}, use_global_device_ids=true | all-gather | bytes 331776 | tf_op jit(solution)/shard_map/all_gather | solution.py:258
  (423 shorter events, 289.5 us)
Async XLA Ops:
  7.2 113.9 %all-reduce.6.cloned.1.call-start = ((), (), s32[]{:S(2)}) async-start(), calls=%async_computation.31 | async-start | bytes 589824
  44.8 79.0 %copy-start.29 = (bf16[2,96,3072]{2,1,0:T(8,128)(2,1)S(1)}, bf16[2,96,3072]{2,1,0:T(8,128)(2,1)}, u32[]{:S(2)}) copy-start(bf16[2,96,3072]{2,1,0:T(8,128)(2,1)} %param.21) | copy-start | bytes 3538948
  48.8 121.1 %all-gather.13.cloned.1.call-start = ((), (), s32[]{:S(2)}) async-start(), calls=%async_computation.13 | async-start | bytes 1966080 | tf_op jit(solution)/shard_map/all_gather | solution.py:159
  123.7 88.8 %all-gather.15.cloned.1.call-start = ((), (), s32[]{:S(2)}) async-start(), calls=%async_computation.14 | async-start | bytes 3981312 | tf_op jit(solution)/shard_map/all_gather | solution.py:117
  186.8 10.8 %all-to-all-start = ((bf16[4,256,192]{1,2,0:T(8,128)(2,1)}), bf16[4,256,192]{1,2,0:T(8,128)(2,1)S(1)}, u32[]{:S(2)}, u32[]{:S(2)}) async-start(bf16[4,256,192]{1,2,0:T(8,128)(2,1)} %copy.126), calls=%async_computation | async-start | bytes 786432 | tf_op jit(solution)/shard_map/all_to_all | solution.py:163
  190.2 44.7 %all-gather.17.cloned.1.call-start = ((), (), s32[]{:S(2)}) async-start(), calls=%async_computation.15 | async-start | bytes 1966080 | tf_op jit(solution)/shard_map/all_gather | solution.py:168
  216.4 66.4 %reduce-scatter.13.cloned.1.call-start = ((), (), s32[]{:S(2)}) async-start(), calls=%async_computation.16 | async-start | bytes 3932160 | tf_op jit(solution)/shard_map/reduce_scatter | solution.py:172
  244.8 77.9 %all-gather.19.cloned.1.call-start = ((), (), s32[]{:S(2)}) async-start(), calls=%async_computation.17 | async-start | bytes 1966080 | tf_op jit(solution)/shard_map/all_gather | solution.py:159
  285.4 87.2 %all-gather.21.cloned.1.call-start = ((), (), s32[]{:S(2)}) async-start(), calls=%async_computation.18 | async-start | bytes 3981312 | tf_op jit(solution)/shard_map/all_gather | solution.py:117
  340.0 32.6 %all-to-all-start.1 = ((bf16[4,256,192]{1,2,0:T(8,128)(2,1)}), bf16[4,256,192]{1,2,0:T(8,128)(2,1)S(1)}, u32[]{:S(2)}, u32[]{:S(2)}) async-start(bf16[4,256,192]{1,2,0:T(8,128)(2,1)} %copy.131), calls=%async_computation.2 | async-start | bytes 786432 | tf_op jit(solution)/shard_map/all_to_all | solution.py:163
  343.5 51.7 %all-gather.23.cloned.1.call-start = ((), (), s32[]{:S(2)}) async-start(), calls=%async_computation.19 | async-start | bytes 1966080 | tf_op jit(solution)/shard_map/all_gather | solution.py:168
  376.7 40.3 %all-gather.25.cloned.1.call-start = ((), (), s32[]{:S(2)}) async-start(), calls=%async_computation.21 | async-start | bytes 1966080 | tf_op jit(solution)/shard_map/all_gather | solution.py:189
  377.6 88.5 %reduce-scatter.17.cloned.1.call-start = ((), (), s32[]{:S(2)}) async-start(), calls=%async_computation.22 | async-start | bytes 3932160 | tf_op jit(solution)/shard_map/reduce_scatter | solution.py:193
  428.0 78.5 %reduce-scatter.15.cloned.1.call-start = ((), (), s32[]{:S(2)}) async-start(), calls=%async_computation.20 | async-start | bytes 3932160 | tf_op jit(solution)/shard_map/reduce_scatter | solution.py:172
  434.1 157.3 %reduce-scatter.19.cloned.1.call-start = ((), (), s32[]{:S(2)}) async-start(), calls=%async_computation.23 | async-start | bytes 3932160 | tf_op jit(solution)/shard_map/reduce_scatter | solution.py:207
  553.4 61.7 %all-gather.27.cloned.1.call-start = ((), (), s32[]{:S(2)}) async-start(), calls=%async_computation.24 | async-start | bytes 1966080 | tf_op jit(solution)/shard_map/all_gather | solution.py:189
  595.3 68.9 %reduce-scatter.21.cloned.1.call-start = ((), (), s32[]{:S(2)}) async-start(), calls=%async_computation.25 | async-start | bytes 3932160 | tf_op jit(solution)/shard_map/reduce_scatter | solution.py:193
  626.2 135.1 %reduce-scatter.27.cloned.1.call-start = ((), (), s32[]{:S(2)}) async-start(), calls=%async_computation.30 | async-start | bytes 5087232
  643.2 162.8 %reduce-scatter.23.cloned.1.call-start = ((), (), s32[]{:S(2)}) async-start(), calls=%async_computation.26 | async-start | bytes 3932160 | tf_op jit(solution)/shard_map/reduce_scatter | solution.py:207
  710.9 188.8 %reduce-scatter.25.cloned.1.call-start = ((), (), s32[]{:S(2)}) async-start(), calls=%async_computation.29 | async-start | bytes 5087232
  727.4 78.6 %copy-start.48 = (f32[256]{0:T(256)S(1)}, f32[256]{0:T(256)}, u32[]{:S(2)}) copy-start(f32[256]{0:T(256)} %copy-done.47) | copy-start | bytes 3076
  727.4 239.0 %all-reduce.4.cloned.1.call-start = ((), (), s32[]{:S(2)}) async-start(), calls=%async_computation.27 | async-start | bytes 786432 | tf_op jit(solution)/shard_map/psum | solution.py:249
  902.9 65.5 %all-gather.29.cloned.1.call-start = ((), (), s32[]{:S(2)}) async-start(), calls=%async_computation.28 | async-start | bytes 4177920 | tf_op jit(solution)/shard_map/all_gather | solution.py:239
  953.1 11.6 %all-to-all-start.4 = ((f32[8,1,96]{2,1,0:T(1,128)}), f32[8,1,96]{2,1,0:T(1,128)S(1)}, u32[]{:S(2)}, u32[]{:S(2)}) async-start(f32[8,1,96]{2,1,0:T(1,128)} %bitcast.68), calls=%async_computation.10 | async-start | bytes 8192 | tf_op jit(solution)/shard_map/all_to_all | solution.py:285
  (66 other events, 1097.1 us)
Sparse Core Ops, SparseCore 0:
  49.0 72.1 all-reduce.5
  123.8 18.6 all-gather.12
  145.3 67.1 all-gather.14
  216.5 18.3 all-gather.16
  244.9 37.8 reduce-scatter.12
  285.5 19.6 all-gather.18
  307.9 64.5 all-gather.20
  376.8 18.3 all-gather.22
  397.3 19.6 all-gather.24
  428.2 37.8 reduce-scatter.16
  468.6 37.8 reduce-scatter.14
  553.5 37.8 reduce-scatter.18
  595.4 19.6 all-gather.26
  626.3 37.8 reduce-scatter.20
  667.7 93.5 reduce-scatter.26
  764.2 37.6 reduce-scatter.22
  805.4 94.2 reduce-scatter.24
  903.1 32.5 all-reduce.3
  937.8 29.6 all-gather.28
where the time goes:
time: 1020 us; the launch traced here: 1010 us
  waiting for transfers between devices  487 us (48%)
  blocking collectives  203 us (20%)
  matrix products  144 us (14%)
  local copies, waits for them, and re-layouts  90.3 us (9%)
  other arithmetic  55.2 us (5%)
  between operations  15.6 us (2%)
  starting transfers between devices  13.8 us (1%)
    unnamed x22, waiting for transfers between devices  196 us
    reduce_scatter x2, waiting for transfers between devices, per_device(): lax.psum_scatter(feed, 'seq', scatter_dimension=0, tiled=True) + down_b[l]  76.8 us
    all_gather x2, blocking collectives, per_device(): w_qkv.append(lax.all_gather(q_part, 'fsdp', axis=0, tiled=True))  67.3 us
    reduce_scatter x2, waiting for transfers between devices, per_device(): lax.psum_scatter(mm_nt(g_up, w_rest[l][:, :fw]), 'seq', scatter_dimension...  52.9 us
    all_gather x2, waiting for transfers between devices, per_device(): w_rest.append(lax.all_gather(rest, 'fsdp', axis=0, tiled=True))  43.6 us
    psum x1, blocking collectives, per_device(): bias = lax.psum(jnp.stack(bias_grads), ('fsdp', 'seq'))  40.9 us
    reduce_scatter x2, waiting for transfers between devices, per_device(): lax.psum_scatter(mm_nt(g_qkv, w_qkv[l]), 'seq', scatter_dimension=0, tile...  38 us
    all_gather x2, waiting for transfers between devices, per_device(): g_feed_all = lax.all_gather(g_feed, 'seq', axis=0, tiled=True)  36.6 us
  transfers between devices with their start and end apart: 22, of which 16 were waited for; matrix products, arithmetic and copies ran while one was open for 15% of the time, Pallas kernels for 0%

commit v1 on v0

--- a/solution.py
+++ b/solution.py
@@ -9,6 +9,12 @@
 HIGHEST = lax.Precision.HIGHEST
 F32 = jnp.float32
 BF16 = jnp.bfloat16
+
+
+def gather_and_add(value, mesh_axis):
+    shards = lax.all_gather(value, mesh_axis, axis=0, tiled=False)
+    total = shards.sum(axis=0)
+    return total
 
 
 def normalize(values):
@@ -247,7 +253,7 @@
     grad_qkv = shared[..., fw + width :].reshape(ns, layers, rows, 3, hc).transpose(1, 2, 3, 0, 4)
     grad_qkv = grad_qkv.reshape(layers, rows, 3 * width)
     grad_out = lax.psum(red[:, :, fw + width : fw + 2 * width], "seq").astype(F32)
-    bias = lax.psum(jnp.stack(bias_grads), ("fsdp", "seq"))
+    bias = gather_and_add(jnp.stack(bias_grads), ("fsdp", "seq"))
     bias = lax.dynamic_index_in_dim(bias, f, 1, keepdims=False)
     cuts = [qv_bias.shape[1], out_bias.shape[1], up_bias.shape[1], down_bias.shape[1]]
     grad_bias, at = ([], 0)

time: 1020 us -> 1080 us (1.059)
  waiting for transfers between devices: 487 us -> 587 us
  blocking collectives: 203 us -> 152 us
    all_gather x0 -> x1, waiting for transfers between devices: none -> 56.4 us  [gather_and_add(): shards = lax.all_gather(value, mesh_axis, axis=0, tiled=False)]
    psum x1 -> x0, blocking collectives: 40.9 us -> none  [per_device(): bias = lax.psum(jnp.stack(bias_grads), ('fsdp', 'seq'))]
    reduce_scatter x2, waiting for transfers between devices: 38 us -> 74.5 us  [per_device(): lax.psum_scatter(mm_nt(g_qkv, w_qkv[l]), 'seq', scatter_dimension=0, tile...]
    unnamed x22 -> x23, waiting for transfers between devices: 196 us -> 197 us
    unnamed x158 -> x155, local copies, waits for them, and re-layouts: 27.4 us -> 28.7 us
  transfers between devices with their start and end apart: 22 -> 24, of which waited for: 16 -> 19; matrix products, arithmetic and copies ran while one was open for 15% -> 15% of each run, Pallas kernels for 0% -> 0%
where the time goes in v1:
time: 1080 us; the launch traced here: 1070 us
  waiting for transfers between devices  587 us (54%)
  blocking collectives  152 us (14%)
  matrix products  147 us (14%)
  local copies, waits for them, and re-layouts  92.4 us (9%)
  other arithmetic  53.8 us (5%)
  starting transfers between devices  17.4 us (2%)
  between operations  15.9 us (1%)
    unnamed x23, waiting for transfers between devices  197 us
    reduce_scatter x2, waiting for transfers between devices, per_device(): lax.psum_scatter(feed, 'seq', scatter_dimension=0, tiled=True) + down_b[l]  76.8 us
    reduce_scatter x2, waiting for transfers between devices, per_device(): lax.psum_scatter(mm_nt(g_qkv, w_qkv[l]), 'seq', scatter_dimension=0, tile...  74.5 us
    all_gather x2, blocking collectives, per_device(): w_qkv.append(lax.all_gather(q_part, 'fsdp', axis=0, tiled=True))  67.5 us
    all_gather x1, waiting for transfers between devices, gather_and_add(): shards = lax.all_gather(value, mesh_axis, axis=0, tiled=False)  56.4 us
    reduce_scatter x2, waiting for transfers between devices, per_device(): lax.psum_scatter(mm_nt(g_up, w_rest[l][:, :fw]), 'seq', scatter_dimension...  53 us
    all_gather x2, waiting for transfers between devices, per_device(): w_rest.append(lax.all_gather(rest, 'fsdp', axis=0, tiled=True))  43.5 us
    all_gather x2, waiting for transfers between devices, per_device(): g_feed_all = lax.all_gather(g_feed, 'seq', axis=0, tiled=True)  36.6 us
  transfers between devices with their start and end apart: 24, of which 19 were waited for; matrix products, arithmetic and copies ran while one was open for 15% of the time, Pallas kernels for 0%

profile of v1, /device:TPU:0, one launch (start us, length us, event | category | flops | bytes accessed | tf_op | source)
XLA Modules:
  0.0 1065.9 jit_solution(8272478113875984896)
XLA Ops:
  12.4 32.4 %all-gather.3 = bf16[8,1,3456]{2,1,0:T(2,128)(2,1)S(1)} all-gather(bf16[1,1,3456]{2,1,0:T(2,128)(2,1)S(1)} %reshape.392), channel_id=2, replica_groups=mesh['fsdp'=8,'seq'=4] {'fsdp'}, dimensions={0}, use_global_device_ids=true | all-gather | bytes 62208 | tf_op jit(solution)/shard_map/all_gather | solution.py:137
  50.2 71.0 %all-reduce.6.cloned.1.call-done = f32[8,2,4608]{2,1,0:T(2,128)} async-done(((f32[8,2,4608]{2,1,0:T(2,128)}), f32[8,2,4608]{2,1,0:T(2,128)}) %all-reduce.6.cloned.1.call-update) | async-done | bytes 294928
  135.6 34.4 %all_gather.57 = bf16[768,576]{1,0:T(8,128)(2,1)S(1)} all-gather(bf16[96,576]{1,0:T(8,128)(2,1)S(1)} %copy.153), channel_id=1, replica_groups=mesh['fsdp'=8,'seq'=4] {'fsdp'}, dimensions={0}, use_global_device_ids=true | all-gather | bytes 995328 | tf_op jit(solution)/shard_map/all_gather | solution.py:121
  197.6 14.9 %all-gather.17.cloned.1.call-done = bf16[768,2304]{1,0:T(8,128)(2,1)} async-done(((bf16[96,2304]{1,0:T(8,128)(2,1)}), bf16[768,2304]{1,0:T(8,128)(2,1)}) %all-gather.17.cloned.1.call-update) | async-done | bytes 3538960 | tf_op jit(solution)/shard_map/all_gather | solution.py:123
  216.7 18.2 %all-gather.19.cloned.1.call-done = bf16[1024,768]{1,0:T(8,128)(2,1)} async-done(((bf16[256,768]{1,0:T(8,128)(2,1)}), bf16[1024,768]{1,0:T(8,128)(2,1)}) %all-gather.19.cloned.1.call-update) | async-done | bytes 1572880 | tf_op jit(solution)/shard_map/all_gather | solution.py:174
  244.9 37.9 %reduce-scatter.13.cloned.1.call-done = f32[256,768]{1,0:T(8,128)} async-done(((f32[1024,768]{1,0:T(8,128)}), f32[256,768]{1,0:T(8,128)}) %reduce-scatter.13.cloned.1.call-update) | async-done | bytes 786448 | tf_op jit(solution)/shard_map/reduce_scatter | solution.py:178
  289.8 33.0 %all_gather.61 = bf16[768,576]{1,0:T(8,128)(2,1)S(1)} all-gather(bf16[96,576]{1,0:T(8,128)(2,1)S(1)} %copy.159), channel_id=1, replica_groups=mesh['fsdp'=8,'seq'=4] {'fsdp'}, dimensions={0}, use_global_device_ids=true | all-gather | bytes 995328 | tf_op jit(solution)/shard_map/all_gather | solution.py:121
  326.4 6.9 fusion.2
  344.0 28.6 %all-gather.23.cloned.1.call-done = bf16[768,2304]{1,0:T(8,128)(2,1)} async-done(((bf16[96,2304]{1,0:T(8,128)(2,1)}), bf16[768,2304]{1,0:T(8,128)(2,1)}) %all-gather.23.cloned.1.call-update) | async-done | bytes 3538960 | tf_op jit(solution)/shard_map/all_gather | solution.py:123
  377.7 17.5 %all-gather.25.cloned.1.call-done = bf16[1024,768]{1,0:T(8,128)(2,1)} async-done(((bf16[256,768]{1,0:T(8,128)(2,1)}), bf16[1024,768]{1,0:T(8,128)(2,1)}) %all-gather.25.cloned.1.call-update) | async-done | bytes 1572880 | tf_op jit(solution)/shard_map/all_gather | solution.py:174
  400.0 17.0 %all-gather.27.cloned.1.call-done = bf16[1024,768]{1,0:T(8,128)(2,1)} async-done(((bf16[256,768]{1,0:T(8,128)(2,1)}), bf16[1024,768]{1,0:T(8,128)(2,1)}) %all-gather.27.cloned.1.call-update) | async-done | bytes 1572880 | tf_op jit(solution)/shard_map/all_gather | solution.py:195
  434.2 31.9 %reduce-scatter.17.cloned.1.call-done = f32[256,768]{1,0:T(8,128)} async-done(((f32[1024,768]{1,0:T(8,128)}), f32[256,768]{1,0:T(8,128)}) %reduce-scatter.17.cloned.1.call-update) | async-done | bytes 786448 | tf_op jit(solution)/shard_map/reduce_scatter | solution.py:199
  467.7 38.9 %reduce-scatter.15.cloned.1.call-done = f32[256,768]{1,0:T(8,128)} async-done(((f32[1024,768]{1,0:T(8,128)}), f32[256,768]{1,0:T(8,128)}) %reduce-scatter.15.cloned.1.call-update) | async-done | bytes 786448 | tf_op jit(solution)/shard_map/reduce_scatter | solution.py:178
  511.6 10.2 all_to_all.80
  523.1 7.5 convert_reduce_fusion.5
  553.5 38.0 %reduce-scatter.19.cloned.1.call-done = f32[256,768]{1,0:T(8,128)} async-done(((f32[1024,768]{1,0:T(8,128)}), f32[256,768]{1,0:T(8,128)}) %reduce-scatter.19.cloned.1.call-update) | async-done | bytes 786448 | tf_op jit(solution)/shard_map/reduce_scatter | solution.py:213
  595.6 19.6 %all-gather.29.cloned.1.call-done = bf16[1024,768]{1,0:T(8,128)(2,1)} async-done(((bf16[256,768]{1,0:T(8,128)(2,1)}), bf16[1024,768]{1,0:T(8,128)(2,1)}) %all-gather.29.cloned.1.call-update) | async-done | bytes 1572880 | tf_op jit(solution)/shard_map/all_gather | solution.py:195
  643.4 21.0 %reduce-scatter.21.cloned.1.call-done = f32[256,768]{1,0:T(8,128)} async-done(((f32[1024,768]{1,0:T(8,128)}), f32[256,768]{1,0:T(8,128)}) %reduce-scatter.21.cloned.1.call-update) | async-done | bytes 786448 | tf_op jit(solution)/shard_map/reduce_scatter | solution.py:199
  731.3 30.2 %reduce-scatter.27.cloned.1.call-done = bf16[96,2880]{1,0:T(8,128)(2,1)} async-done(((bf16[768,2880]{1,0:T(8,128)(2,1)}), bf16[96,2880]{1,0:T(8,128)(2,1)}) %reduce-scatter.27.cloned.1.call-update) | async-done | bytes 552976
  762.9 56.4 %all-gather.33.cloned.1.call-done = f32[64,8,768]{2,1,0:T(8,128)} async-done(((f32[2,8,768]{2,1,0:T(8,128)}), f32[64,8,768]{2,1,0:T(8,128)}) %all-gather.33.cloned.1.call-update) | async-done | bytes 1572880 | tf_op jit(solution)/shard_map/all_gather | solution.py:15
  822.6 36.5 %reduce-scatter.23.cloned.1.call-done = f32[256,768]{1,0:T(8,128)} async-done(((f32[1024,768]{1,0:T(8,128)}), f32[256,768]{1,0:T(8,128)}) %reduce-scatter.23.cloned.1.call-update) | async-done | bytes 786448 | tf_op jit(solution)/shard_map/reduce_scatter | solution.py:213
  860.7 95.8 %reduce-scatter.25.cloned.1.call-done = bf16[96,2880]{1,0:T(8,128)(2,1)} async-done(((bf16[768,2880]{1,0:T(8,128)(2,1)}), bf16[96,2880]{1,0:T(8,128)(2,1)}) %reduce-scatter.25.cloned.1.call-update) | async-done | bytes 552976
  965.3 11.1 %psum.14 = f32[1,2,4608]{2,1,0:T(2,128)S(1)} all-reduce(f32[1,2,4608]{2,1,0:T(2,128)S(1)} %maximum_bitcast_fusion), channel_id=1, replica_groups=mesh['fsdp'=8,'seq'=4] {'seq'}, use_global_device_ids=true, to_apply=%region_39.40 | all-reduce | flops 9216 | bytes 73728 | tf_op jit(solution)/shard_map/psum | solution.py:263
  976.3 31.0 %all_gather.67 = f32[8,2,4608]{2,1,0:T(2,128)S(1)} all-gather(f32[1,2,4608]{2,1,0:T(2,128)S(1)} %psum.14), channel_id=1, replica_groups=mesh['fsdp'=8,'seq'=4] {'fsdp'}, dimensions={0}, use_global_device_ids=true | all-gather | bytes 331776 | tf_op jit(solution)/shard_map/all_gather | solution.py:264
  (421 shorter events, 310.1 us)
Async XLA Ops:
  7.2 113.9 %all-reduce.6.cloned.1.call-start = ((), (), s32[]{:S(2)}) async-start(), calls=%async_computation.32 | async-start | bytes 589824
  48.8 121.1 %all-gather.15.cloned.1.call-start = ((), (), s32[]{:S(2)}) async-start(), calls=%async_computation.13 | async-start | bytes 1966080 | tf_op jit(solution)/shard_map/all_gather | solution.py:165
  123.7 88.8 %all-gather.17.cloned.1.call-start = ((), (), s32[]{:S(2)}) async-start(), calls=%async_computation.14 | async-start | bytes 3981312 | tf_op jit(solution)/shard_map/all_gather | solution.py:123
  186.8 10.8 %all-to-all-start = ((bf16[4,256,192]{1,2,0:T(8,128)(2,1)}), bf16[4,256,192]{1,2,0:T(8,128)(2,1)S(1)}, u32[]{:S(2)}, u32[]{:S(2)}) async-start(bf16[4,256,192]{1,2,0:T(8,128)(2,1)} %copy.156), calls=%async_computation | async-start | bytes 786432 | tf_op jit(solution)/shard_map/all_to_all | solution.py:169
  190.2 44.7 %all-gather.19.cloned.1.call-start = ((), (), s32[]{:S(2)}) async-start(), calls=%async_computation.15 | async-start | bytes 1966080 | tf_op jit(solution)/shard_map/all_gather | solution.py:174
  216.4 66.4 %reduce-scatter.13.cloned.1.call-start = ((), (), s32[]{:S(2)}) async-start(), calls=%async_computation.16 | async-start | bytes 3932160 | tf_op jit(solution)/shard_map/reduce_scatter | solution.py:178
  244.8 78.1 %all-gather.21.cloned.1.call-start = ((), (), s32[]{:S(2)}) async-start(), calls=%async_computation.17 | async-start | bytes 1966080 | tf_op jit(solution)/shard_map/all_gather | solution.py:165
  285.4 87.2 %all-gather.23.cloned.1.call-start = ((), (), s32[]{:S(2)}) async-start(), calls=%async_computation.18 | async-start | bytes 3981312 | tf_op jit(solution)/shard_map/all_gather | solution.py:123
  340.2 32.4 %all-to-all-start.1 = ((bf16[4,256,192]{1,2,0:T(8,128)(2,1)}), bf16[4,256,192]{1,2,0:T(8,128)(2,1)S(1)}, u32[]{:S(2)}, u32[]{:S(2)}) async-start(bf16[4,256,192]{1,2,0:T(8,128)(2,1)} %copy.161), calls=%async_computation.2 | async-start | bytes 786432 | tf_op jit(solution)/shard_map/all_to_all | solution.py:169
  343.6 51.5 %all-gather.25.cloned.1.call-start = ((), (), s32[]{:S(2)}) async-start(), calls=%async_computation.19 | async-start | bytes 1966080 | tf_op jit(solution)/shard_map/all_gather | solution.py:174
  376.7 40.3 %all-gather.27.cloned.1.call-start = ((), (), s32[]{:S(2)}) async-start(), calls=%async_computation.21 | async-start | bytes 1966080 | tf_op jit(solution)/shard_map/all_gather | solution.py:195
  377.6 88.6 %reduce-scatter.17.cloned.1.call-start = ((), (), s32[]{:S(2)}) async-start(), calls=%async_computation.22 | async-start | bytes 3932160 | tf_op jit(solution)/shard_map/reduce_scatter | solution.py:199
  428.1 78.5 %reduce-scatter.15.cloned.1.call-start = ((), (), s32[]{:S(2)}) async-start(), calls=%async_computation.20 | async-start | bytes 3932160 | tf_op jit(solution)/shard_map/reduce_scatter | solution.py:178
  434.1 157.4 %reduce-scatter.19.cloned.1.call-start = ((), (), s32[]{:S(2)}) async-start(), calls=%async_computation.23 | async-start | bytes 3932160 | tf_op jit(solution)/shard_map/reduce_scatter | solution.py:213
  553.5 61.7 %all-gather.29.cloned.1.call-start = ((), (), s32[]{:S(2)}) async-start(), calls=%async_computation.24 | async-start | bytes 1966080 | tf_op jit(solution)/shard_map/all_gather | solution.py:195
  595.4 69.0 %reduce-scatter.21.cloned.1.call-start = ((), (), s32[]{:S(2)}) async-start(), calls=%async_computation.25 | async-start | bytes 3932160 | tf_op jit(solution)/shard_map/reduce_scatter | solution.py:199
  626.4 135.1 %reduce-scatter.27.cloned.1.call-start = ((), (), s32[]{:S(2)}) async-start(), calls=%async_computation.31 | async-start | bytes 5087232
  671.1 10.8 %all-to-all-start.3 = ((bf16[256,4,192]{0,2,1:T(8,128)(2,1)}), bf16[256,4,192]{0,2,1:T(8,128)(2,1)S(1)}, u32[]{:S(2)}, u32[]{:S(2)}) async-start(bf16[256,4,192]{0,2,1:T(8,128)(2,1)} %bitcast.53), calls=%async_computation.8 | async-start | bytes 786432 | tf_op jit(solution)/shard_map/all_to_all | solution.py:209
  674.6 144.7 %all-gather.33.cloned.1.call-start = ((), (), s32[]{:S(2)}) async-start(), calls=%async_computation.29 | async-start | bytes 1622016 | tf_op jit(solution)/shard_map/all_gather | solution.py:15
  706.5 152.6 %reduce-scatter.23.cloned.1.call-start = ((), (), s32[]{:S(2)}) async-start(), calls=%async_computation.26 | async-start | bytes 3932160 | tf_op jit(solution)/shard_map/reduce_scatter | solution.py:213
  714.6 241.9 %reduce-scatter.25.cloned.1.call-start = ((), (), s32[]{:S(2)}) async-start(), calls=%async_computation.30 | async-start | bytes 5087232
  731.1 292.3 %all-reduce.4.cloned.1.call-start = ((), (), s32[]{:S(2)}) async-start(), calls=%async_computation.27 | async-start | bytes 786432 | tf_op jit(solution)/shard_map/psum | solution.py:255
  959.8 65.6 %all-gather.31.cloned.1.call-start = ((), (), s32[]{:S(2)}) async-start(), calls=%async_computation.28 | async-start | bytes 4177920 | tf_op jit(solution)/shard_map/all_gather | solution.py:245
  1009.9 11.6 %all-to-all-start.4 = ((f32[8,1,96]{2,1,0:T(1,128)}), f32[8,1,96]{2,1,0:T(1,128)S(1)}, u32[]{:S(2)}, u32[]{:S(2)}) async-start(f32[8,1,96]{2,1,0:T(1,128)} %bitcast.68), calls=%async_computation.10 | async-start | bytes 8192 | tf_op jit(solution)/shard_map/all_to_all | solution.py:291
  (66 other events, 1387.5 us)
Sparse Core Ops, SparseCore 0:
  49.0 72.1 all-reduce.5
  123.8 18.6 all-gather.14
  145.3 67.1 all-gather.16
  216.5 18.3 all-gather.18
  244.9 37.8 reduce-scatter.12
  285.5 19.6 all-gather.20
  307.9 64.5 all-gather.22
  376.8 18.3 all-gather.24
  397.3 19.6 all-gather.26
  428.2 37.8 reduce-scatter.16
  468.7 37.8 reduce-scatter.14
  553.6 37.8 reduce-scatter.18
  595.5 19.6 all-gather.28
  626.5 37.8 reduce-scatter.20
  667.9 93.5 reduce-scatter.26
  764.7 54.4 all-gather.32
  822.2 36.8 reduce-scatter.22
  862.6 93.8 reduce-scatter.24
  959.9 32.6 all-reduce.3
  994.5 29.6 all-gather.30
